TPU v7x, 32 devices: a whole 2x2x4 slice. The times are simulated.
32 devices in a mesh: dp: 2 (over x), ep: 4 (over z), tp: 4 (over y, core).
Axes of the slice: x: 2, y: 2, z: 4, core: 2. Of those that a mesh axis runs over, the one named last changes fastest.
Arguments:
- x_in: bfloat16 [32768, 2048], P(('dp', 'ep')), parts along dimension 0
- expert_ids: int32 [32768, 2], P(('dp', 'ep')), parts along dimension 0
- gate_vals: float32 [32768, 2], P(('dp', 'ep')), parts along dimension 0
- w_gate: bfloat16 [8, 2048, 5632], P('ep', None, 'tp')
- w_up: bfloat16 [8, 2048, 5632], P('ep', None, 'tp')
- w_down: bfloat16 [8, 5632, 2048], P('ep', 'tp')
Outputs:
- output: bfloat16 [32768, 2048], P(('dp', 'ep')), parts along dimension 0
There are 2 independent parts. A program takes and returns all parts, laid end to end along the dimension named above; an argument that names none is the same for every part.
All inputs are finite; a program needn't handle non-finite values.
Results may differ from a plain program's by a relative error of at most 0.00950133.
Values are sent between devices in bfloat16 or wider.
A program may use at most 1 GiB of HBM per device.

v0:
```python
import jax
import jax.numpy as jnp
from jax import lax
from jax.sharding import PartitionSpec as P

CAP_NUM = 5
CAP_DEN = 4


def local_routing(expert_ids, n_experts, capacity):
    tokens, n_top = expert_ids.shape
    flat_ids = expert_ids.reshape(tokens * n_top)
    onehot = (flat_ids[:, None] == jnp.arange(n_experts, dtype=jnp.int32)[None, :]).astype(jnp.int32)
    slots = jnp.sum((jnp.cumsum(onehot, axis=0) - onehot) * onehot, axis=1)
    flat_slot = jnp.where(slots < capacity, flat_ids * capacity + slots, n_experts * capacity)
    token_num = jnp.broadcast_to(jnp.arange(tokens, dtype=jnp.int32)[:, None], (tokens, n_top)).reshape(tokens * n_top)
    slot_owner = jnp.full((n_experts * capacity + 1,), tokens, jnp.int32).at[flat_slot].set(token_num)
    return slot_owner[: n_experts * capacity].reshape(n_experts, capacity), flat_slot.reshape(tokens, n_top)


def solution(mesh):
    n_ep = mesh.shape['ep']
    n_tp = mesh.shape['tp']
    row_spec = P(('dp', 'ep'), None)

    def device_body(x_loc, ids_loc, gates_loc, wg_loc, wu_loc, wd_loc):
        tokens, d_model = x_loc.shape
        n_top = ids_loc.shape[1]
        local_experts = wg_loc.shape[0]
        n_experts = local_experts * n_ep
        capacity = CAP_NUM * n_top * tokens // (CAP_DEN * n_experts)
        slot_share = capacity // n_tp
        slot_owner, flat_slot = local_routing(ids_loc, n_experts, capacity)
        my_owner = lax.dynamic_slice_in_dim(slot_owner, lax.axis_index('tp') * slot_share, slot_share, axis=1)
        outgoing = jnp.take(x_loc, my_owner, axis=0, mode='fill', fill_value=0)
        outgoing = outgoing.reshape(n_ep, local_experts, slot_share, d_model)
        arrived = lax.all_to_all(outgoing, 'ep', 0, 2, tiled=True).reshape(local_experts, n_ep * slot_share, d_model)
        gathered = lax.all_gather(arrived, 'tp', axis=1, tiled=True)
        h_gate = jnp.einsum('erd,edf->erf', gathered, wg_loc, preferred_element_type=jnp.float32)
        h_up = jnp.einsum('erd,edf->erf', gathered, wu_loc, preferred_element_type=jnp.float32)
        hidden = (jax.nn.silu(h_gate) * h_up).astype(jnp.bfloat16)
        part_out = jnp.einsum('erf,efd->erd', hidden, wd_loc, preferred_element_type=jnp.float32).astype(jnp.bfloat16)
        part_out = part_out.reshape(local_experts, n_tp, n_ep * slot_share, d_model)
        pieces = lax.all_to_all(part_out, 'tp', 1, 1, tiled=True)
        y_mine = jnp.sum(pieces, axis=1, dtype=jnp.float32).astype(jnp.bfloat16)
        returned = lax.all_to_all(y_mine.reshape(local_experts, n_ep, slot_share, d_model), 'ep', 1, 0, tiled=True)
        returned = returned.reshape(n_experts, slot_share, d_model)
        y_all = lax.all_gather(returned, 'tp', axis=1, tiled=True).reshape(n_experts * capacity, d_model)
        picked = jnp.take(y_all, flat_slot, axis=0, mode='fill', fill_value=0)
        return jnp.sum(picked * gates_loc[:, :, None], axis=1).astype(jnp.bfloat16)

    return jax.shard_map(device_body, mesh=mesh,
                         in_specs=(row_spec, row_spec, row_spec, P('ep', None, 'tp'), P('ep', None, 'tp'), P('ep', 'tp', None)),
                         out_specs=row_spec, check_vma=False)
```

profile of v0, /device:TPU:0, one launch (start us, length us, event | category | flops | bytes accessed | tf_op | source)
XLA Modules:
  0.0 2235.1 jit_solution(11608318687940783329)
XLA Ops:
  6.5 0.0 all-gather.3.cloned.1.call-start
  6.5 1.4 copy.23
  7.9 0.0 copy-start
  7.9 1.2 eq.29
  9.2 1.2 eq.25
  10.4 1.5 broadcast_multiply_fusion
  11.9 2.4 reduce-window.6
  14.3 0.3 slice_reduce_fusion
  14.6 0.2 reduce-window.9
  14.8 0.1 add_bitcast_fusion
  15.0 3.0 mul.37
  18.0 1.5 broadcast_in_dim.48
  19.5 2.7 reshape.120
  22.2 0.2 fusion.2
  22.4 0.0 copy-start.2
  22.4 0.1 compare_select_fusion.1
  22.5 30.9 %scatter_custom_fusion = s32[10241]{0:T(1024)S(1)} fusion(s32[8192]{0:T(1024)S(1)} %bitcast.48, s32[8192]{0:T(1024)S(1)} %reshape.120, s32[]{:T(128)} %constant.30.clone.1), kind=kCustom, calls=%fused_computation.23 | custom fusion | bytes 40968 | tf_op jit(solution)/shard_map/scatter | solution.py:17
  53.5 0.1 compare_and_fusion.1
  53.6 0.1 reshape.102
  53.7 28.1 %gather_fusion = bf16[2560,2048]{1,0:T(8,128)(2,1)} fusion(bf16[4096,2048]{1,0:T(8,128)(2,1)} %param.6, s32[3072]{0:T(1024)S(1)} %pad_clamp_fusion), kind=kCustom, calls=%fused_computation | custom fusion | bytes 20981760 | tf_op jit(solution)/shard_map/jit(_take)/gather | solution.py:35
  81.8 0.0 copy-done
  81.8 0.0 copy-done.2
  81.8 5.7 broadcast_select_fusion.1
  87.4 234.1 %all_to_all.35 = bf16[4,2,320,2048]{3,2,1,0:T(8,128)(2,1)} all-to-all(bf16[4,2,320,2048]{3,2,1,0:T(8,128)(2,1)S(1)} %broadcast_select_fusion.1), channel_id=1, replica_groups=mesh['dp'=2,'ep'=4,'tp'=4] {'ep'}, dimensions={0} | all-to-all | bytes 20971520 | tf_op jit(solution)/shard_map/all_to_all | solution.py:37
  321.5 10.3 copy.26
  331.8 0.0 all-gather.3.cloned.1.call-update
  331.8 0.2 all-gather.5.cloned.1.call-start
  332.1 251.8 %all-gather.3.cloned.1.call-done = bf16[2,5120,2048]{2,1,0:T(8,128)(2,1)} async-done(((bf16[2,1280,2048]{2,1,0:T(8,128)(2,1)}), bf16[2,5120,2048]{2,1,0:T(8,128)(2,1)}) %all-gather.3.cloned.1.call-update) | async-done | bytes 41943056 | tf_op jit(solution)/shard_map/all_gather | solution.py:38
  583.8 73.8 %fusion.6 = f32[2,5120,1408]{2,1,0:T(8,128)} fusion(bf16[2,5120,2048]{2,1,0:T(8,128)(2,1)} %all-gather.3.cloned.1.call-done, bf16[2,2048,1408]{2,1,0:T(8,128)(2,1)} %param.9), kind=kOutput, calls=%fused_computation.28 | convolution fusion | flops 59055800320 | bytes 111149056 | tf_op jit(solution)/shard_map/erd,edf->erf/dot_general | solution.py:39
  657.6 77.1 %multiply_convert_fusion = bf16[2,5120,1408]{2,1,0:T(8,128)(2,1)} fusion(f32[2,5120,1408]{2,1,0:T(8,128)} %fusion.6, bf16[2,5120,2048]{2,1,0:T(8,128)(2,1)} %all-gather.3.cloned.1.call-done, bf16[2,2048,1408]{2,1,0:T(8,128)(2,1)} %param.10), kind=kOutput, calls=%fused_computation.5 | convolution fusion | flops 59142307840 | bytes 139984896 | tf_op jit(solution)/shard_map/erd,edf->erf/dot_general | solution.py:40
  734.6 74.2 %convolution_convert_fusion = bf16[2,5120,2048]{2,1,0:T(8,128)(2,1)} fusion(bf16[2,5120,1408]{2,1,0:T(8,128)(2,1)} %multiply_convert_fusion, bf16[2,1408,2048]{2,1,0:T(8,128)(2,1)} %param.11), kind=kOutput, calls=%fused_computation.6 | convolution fusion | flops 59076771840 | bytes 82313216 | tf_op jit(solution)/shard_map/erf,efd->erd/dot_general | solution.py:42
  808.8 28.1 %copy.27 = bf16[2,4,1280,2048]{3,2,0,1:T(8,128)(2,1)} copy(bf16[2,4,1280,2048]{3,2,1,0:T(8,128)(2,1)} %bitcast.42) | data formatting | bytes 83886080 | tf_op jit(solution)/shard_map/reshape | solution.py:43
  836.9 474.1 %all_to_all.36 = bf16[2,4,1280,2048]{3,2,0,1:T(8,128)(2,1)} all-to-all(bf16[2,4,1280,2048]{3,2,0,1:T(8,128)(2,1)} %copy.27), channel_id=1, replica_groups=mesh['dp'=2,'ep'=4,'tp'=4] {'tp'}, dimensions={1} | all-to-all | bytes 83886080 | tf_op jit(solution)/shard_map/all_to_all | solution.py:44
  1311.0 20.1 reduce_sum.37
  1331.1 10.2 copy.28
  1341.3 0.0 copy-start.3
  1341.3 236.4 %all_to_all.37 = bf16[2,4,320,2048]{3,2,0,1:T(8,128)(2,1)} all-to-all(bf16[2,4,320,2048]{3,2,0,1:T(8,128)(2,1)} %copy.28), channel_id=1, replica_groups=mesh['dp'=2,'ep'=4,'tp'=4] {'ep'}, dimensions={1} | all-to-all | bytes 20971520 | tf_op jit(solution)/shard_map/all_to_all | solution.py:46
  1577.7 0.0 copy-start.1
  1577.7 0.0 copy-start.4
  1577.7 0.0 all-gather.5.cloned.1.call-update
  1577.7 0.0 copy-done.3
  1577.7 3.4 reduce_sum.35
  1581.1 0.0 copy-done.1
  1581.1 3.8 compare_and_fusion
  1584.9 2.7 reshape.110
  1587.6 0.0 copy-done.4
  1587.6 0.7 copy.29
  1588.3 247.0 %all-gather.5.cloned.1.call-done = bf16[8,1280,2048]{2,1,0:T(8,128)(2,1)} async-done(((bf16[8,320,2048]{2,1,0:T(8,128)(2,1)}), bf16[8,1280,2048]{2,1,0:T(8,128)(2,1)}) %all-gather.5.cloned.1.call-update) | async-done | bytes 41943056 | tf_op jit(solution)/shard_map/all_gather | solution.py:48
  1835.4 190.9 %gather_fusion.1 = bf16[8192,2048]{1,0:T(8,128)(2,1)} fusion(bf16[10240,2048]{1,0:T(8,128)(2,1)} %bitcast.40, s32[8192]{0:T(1024)S(1)} %broadcast_clamp_fusion), kind=kCustom, calls=%fused_computation.1 | custom fusion | bytes 67141632 | tf_op jit(solution)/shard_map/jit(_take)/gather | solution.py:49
  2026.2 52.9 %reshape.109 = bf16[4096,2,2048]{2,1,0:T(2,128)(2,1)} reshape(bf16[8192,2048]{1,0:T(8,128)(2,1)} %gather_fusion.1) | data formatting | bytes 67108864 | tf_op jit(solution)/shard_map/jit(_take)/gather | solution.py:49
  2079.2 148.6 %multiply_reduce_fusion = bf16[4096,2048]{1,0:T(8,128)(2,1)} fusion(bf16[4096,2,2048]{2,1,0:T(2,128)(2,1)} %reshape.109, pred[4096,2]{1,0:T(8,128)(4,1)S(1)} %get-tuple-element.5, f32[4096,2]{1,0:T(8,128)S(1)} %copy.29), kind=kLoop, calls=%fused_computation.3 | loop fusion | flops 58720256 | bytes 50372608 | tf_op jit(solution)/shard_map/reduce_sum | solution.py:50
  (6 shorter events, 0.1 us)
Async XLA Ops:
  6.5 577.3 %all-gather.3.cloned.1.call-start = ((), (), s32[]{:S(2)}) async-start(), calls=%async_computation.3 | async-start | bytes 52428800 | tf_op jit(solution)/shard_map/all_gather | solution.py:38
  7.9 73.8 %copy-start = (s32[4096,2]{1,0:T(8,128)}, s32[4096,2]{1,0:T(8,128)S(1)}, u32[]{:S(2)}) copy-start(s32[4096,2]{1,0:T(8,128)S(1)} %copy.23) | copy-start | bytes 98308
  22.4 59.3 %copy-start.2 = (s32[8192]{0:T(1024)}, s32[8192]{0:T(1024)S(1)}, u32[]{:S(2)}) copy-start(s32[8192]{0:T(1024)S(1)} %fusion.2) | copy-start | bytes 98308
  331.8 1503.5 %all-gather.5.cloned.1.call-start = ((), (), s32[]{:S(2)}) async-start(), calls=%async_computation.4 | async-start | bytes 52428800 | tf_op jit(solution)/shard_map/all_gather | solution.py:48
  1341.3 236.4 %copy-start.3 = (s32[8192]{0:T(1024)S(1)}, s32[8192]{0:T(1024)}, u32[]{:S(2)}) copy-start(s32[8192]{0:T(1024)} %copy-done.2) | copy-start | bytes 98308
  1577.7 3.5 copy-start.1
  1577.7 10.0 copy-start.4
Sparse Core Ops, SparseCore 0:
  332.0 251.8 all-gather.2
  1577.8 257.5 all-gather.4
where the time goes:
time: 2250 us; the launch traced here: 2240 us
  blocking collectives  945 us (42%)
  waiting for transfers between devices  499 us (22%)
  local copies, waits for them, and re-layouts  370 us (16%)
  matrix products  225 us (10%)
  other arithmetic  183 us (8%)
    all_to_all x1, blocking collectives, device_body(): pieces = lax.all_to_all(part_out, 'tp', 1, 1, tiled=True)  474 us
    all_gather x1, waiting for transfers between devices, device_body(): gathered = lax.all_gather(arrived, 'tp', axis=1, tiled=True)  252 us
    all_gather x1, waiting for transfers between devices, device_body(): lax.all_gather(returned, 'tp', axis=1, tiled=True)  247 us
    gather x2, local copies, waits for them, and re-layouts, device_body(): picked = jnp.take(y_all, flat_slot, axis=0, mode='fill', fill_value=0)  244 us
    all_to_all x1, blocking collectives, device_body(): lax.all_to_all(y_mine.reshape(local_experts, n_ep, slot_share, d_model),...  236 us
    all_to_all x1, blocking collectives, device_body(): lax.all_to_all(outgoing, 'ep', 0, 2, tiled=True)  234 us
    reduce_sum x1, other arithmetic, device_body(): return jnp.sum(picked * gates_loc[:, :, None], axis=1).astype(jnp.bfloat16)  149 us
    dot_general x1, matrix products, device_body(): jnp.einsum('erd,edf->erf', gathered, wu_loc, preferred_element_type=jnp.f...  77.1 us
  transfers between devices with their start and end apart: 2, of which 2 were waited for; matrix products, arithmetic and copies ran while one was open for 0% of the time, Pallas kernels for 0%

commit v1 on v0

v1 whole, which is shorter than its diff:
```python
import jax
import jax.numpy as jnp
from jax import lax
from jax.experimental import pallas as pl
from jax.experimental.pallas import tpu as pltpu
from jax.sharding import PartitionSpec as P

CAP_NUM = 5
CAP_DEN = 4
MESH = pl.DeviceIdType.MESH
ANY = pl.BlockSpec(memory_space=pl.ANY)
VMEM_LIMIT = 67_043_328


def slot_numbers(expert_ids, n_experts):
    tokens = expert_ids.shape[0]
    expert = jnp.arange(n_experts, dtype=jnp.int32)[:, None]
    chosen = (expert_ids[:, 0][None, :] == expert) | (expert_ids[:, 1][None, :] == expert)
    lane = 128
    blocks = tokens // lane
    bits = chosen.reshape(n_experts, blocks, lane).astype(jnp.bfloat16)
    before = (jnp.arange(lane)[:, None] < jnp.arange(lane)[None, :]).astype(jnp.bfloat16)
    inside = jnp.einsum('ebi,ij->ebj', bits, before, preferred_element_type=jnp.float32)
    totals = jnp.sum(bits.astype(jnp.float32), axis=2).astype(jnp.bfloat16)
    earlier = (jnp.arange(blocks)[:, None] < jnp.arange(blocks)[None, :]).astype(jnp.bfloat16)
    offsets = jnp.einsum('eb,bc->ec', totals, earlier, preferred_element_type=jnp.float32)
    slots = (inside + offsets[:, :, None]).astype(jnp.int32).reshape(n_experts, tokens)
    return chosen, slots


def flip(bit, mask):
    return bit + mask - 2 * bit * mask


def layer_kernel(rows, wg, wu, wd, ret, arrived, bg, bu, bd,
                 xv, gv, uv, dv, hv, acc, yv,
                 x_sem, w_sem, own_sem,
                 disp_s, disp_r, core_s, core_r, y_s, y_r, x_s, x_r, d1_s, d1_r, d2_s, d2_r, ret_s, ret_r):
    dp, z, tp = lax.axis_index('dp'), lax.axis_index('ep'), lax.axis_index('tp')
    y, c = tp // 2, tp % 2
    n_rows = rows.shape[1]
    ff = wg.shape[2]
    n_ep = rows.shape[0]
    n_tp = 4
    w_in, w_buf, w_vmem = (wg, wu, wd), (bg, bu, bd), (gv, uv, dv)

    def partner(k):
        return 2 * flip(z // 2, 1 - k // 2) + flip(z % 2, ((k + 1) // 2) % 2)

    def remote(src, dst, send, recv, device):
        return pltpu.make_async_remote_copy(src_ref=src, dst_ref=dst, send_sem=send, recv_sem=recv,
                                            device_id=device, device_id_type=MESH)

    peer_core = (dp, z, 2 * y + 1 - c)

    def piece(p, half):
        size = w_in[p // 2].shape[1] // 4
        return pl.ds(pl.multiple_of(half * 2 * size + (p % 2) * size, 16), size)

    def core_copy(a):
        return remote(w_in[a].at[y], w_buf[a].at[0], core_s.at[a], core_r.at[a], peer_core)

    def y_copy(p):
        a, at = p // 2, piece(p, dp)
        return remote(w_in[a].at[1 - y, at], w_buf[a].at[1, at], y_s.at[p], y_r.at[p], (dp, z, 2 * (1 - y) + c))

    def x_copy(p):
        a, at = p // 2, piece(p, dp)
        return remote(w_buf[a].at[1, at], w_buf[a].at[1, at], x_s.at[p], x_r.at[p], (1 - dp, z, tp))

    def d1_copy(p):
        a, at = p // 2, piece(p, dp)
        return remote(w_buf[a].at[1, at], w_buf[a].at[2, at], d1_s.at[p], d1_r.at[p], peer_core)

    def d2_copy(p):
        a, at = p // 2, piece(p, 1 - dp)
        return remote(w_buf[a].at[1, at], w_buf[a].at[2, at], d2_s.at[p], d2_r.at[p], peer_core)

    def dispatch(k):
        return remote(rows.at[partner(k)], arrived.at[k], disp_s.at[k], disp_r.at[k], (dp, partner(k), tp))

    def give_back(k, step):
        quarter = (tp + step) % n_tp
        return remote(yv.at[k, quarter], ret.at[z, tp], ret_s.at[k, step], ret_r.at[k, step],
                      (dp, partner(k), quarter))

    def keep_own():
        return pltpu.make_async_copy(yv.at[n_ep - 1, tp], ret.at[z, tp], own_sem)

    def forward_y(p):
        y_copy(p).wait_recv()
        x_copy(p).start()
        d1_copy(p).start()

    def forward_x(p):
        x_copy(p).wait_recv()
        d2_copy(p).start()

    def load_w(slice_no, slot, a):
        src = w_in[a].at[y] if slice_no == 0 else w_buf[a].at[slice_no - 1]
        return pltpu.make_async_copy(src, w_vmem[a].at[slot], w_sem.at[slot, a])

    def start_w(slice_no, slot):
        for number in range(4):
            @pl.when(slice_no == number)
            def _():
                for a in range(3):
                    load_w(number, slot, a).start()

    def load_x(src, slot):
        return pltpu.make_async_copy(src, xv.at[slot], x_sem.at[slot])

    for k in range(n_ep - 1):
        dispatch(k).start()
    for a in range(3):
        core_copy(a).start()
    for p in range(6):
        y_copy(p).start()
    start_w(0, 0)
    forward_y(0)
    forward_y(1)
    forward_x(0)
    forward_y(2)
    forward_x(1)
    dispatch(0).wait_recv()
    load_x(arrived.at[0], 0).start()

    def step_body(step, carry):
        k, j = step // 4, step % 4
        slot, x_slot = step % 2, k % 2
        last = 4 * n_ep - 1

        @pl.when(step == 0)
        def _():
            for a in range(3):
                core_copy(a).wait_recv()

        @pl.when(step == 2)
        def _():
            for p in range(6):
                d1_copy(p).wait_recv()
                d2_copy(p).wait_recv()

        @pl.when((step != 1) & (step < last))
        def _():
            start_w((j + 1) % 4, 1 - slot)

        @pl.when(j == 0)
        def _():
            load_x(arrived.at[0], x_slot).wait()

        @pl.when((j == 3) & (k < n_ep - 2))
        def _():
            dispatch(k + 1).wait_recv()
            load_x(arrived.at[k + 1], 1 - x_slot).start()

        @pl.when((j == 3) & (k == n_ep - 2))
        def _():
            load_x(rows.at[z], 1 - x_slot).start()

        for a in range(2):
            load_w(0, slot, a).wait()

        def gate_up(at):
            x_now = xv.at[x_slot][...]
            gate = jnp.dot(x_now, gv.at[slot][:, at], preferred_element_type=jnp.float32)
            up = jnp.dot(x_now, uv.at[slot][:, at], preferred_element_type=jnp.float32)
            hv[:, at] = (jax.nn.silu(gate) * up).astype(jnp.bfloat16)

        wide = 256

        def gate_up_loop(t, carry):
            gate_up(pl.ds(pl.multiple_of(t * wide, 128), wide))
            return carry

        lax.fori_loop(0, ff // wide, gate_up_loop, 0)
        if ff % wide:
            gate_up(pl.ds(ff // wide * wide, ff % wide))

        load_w(0, slot, 2).wait()
        quarter_cols = ret.shape[3]

        def down_loop(q, carry):
            at = pl.ds(pl.multiple_of(q * quarter_cols, 128), quarter_cols)
            part = jnp.dot(hv[...], dv.at[slot][:, at], preferred_element_type=jnp.float32)

            @pl.when(j == 0)
            def _():
                acc.at[q][...] = part

            @pl.when((j > 0) & (j < 3))
            def _():
                acc.at[q][...] += part

            @pl.when(j == 3)
            def _():
                yv.at[k, q][...] = (acc.at[q][...] + part).astype(jnp.bfloat16)
            return carry

        lax.fori_loop(0, n_tp, down_loop, 0)

        @pl.when(step == 0)
        def _():
            forward_y(3)
            forward_x(2)

        @pl.when(step == 1)
        def _():
            forward_y(4)
            forward_x(3)
            forward_y(5)
            forward_x(4)
            forward_x(5)
            start_w(2, 1 - slot)

        @pl.when((j == 3) & (k < n_ep - 1))
        def _():
            for q in range(n_tp):
                give_back(k, q).start()
        return carry

    lax.fori_loop(0, 4 * n_ep, step_body, 0)
    keep_own().start()
    for q in range(1, n_tp):
        give_back(n_ep - 1, q).start()

    for k in range(n_ep - 1):
        dispatch(k).wait_send()
    for a in range(3):
        core_copy(a).wait_send()
    for p in range(6):
        y_copy(p).wait_send()
        x_copy(p).wait_send()
        d1_copy(p).wait_send()
        d2_copy(p).wait_send()
    keep_own().wait()
    for k in range(n_ep):
        for q in range(n_tp):
            if k == n_ep - 1 and q == 0:
                continue
            give_back(k, q).wait_send()
    for k in range(n_ep):
        for q in range(n_tp):
            if k == n_ep - 1 and q == 0:
                continue
            source = (tp + n_tp - q) % n_tp
            remote(yv.at[k, source], ret.at[partner(k), source], ret_s.at[k, q], ret_r.at[k, q],
                   (dp, partner(k), source)).wait_recv()


def run_layer(rows, wg, wu, wd):
    n_ep, n_rows, d_model = rows.shape
    ff = wg.shape[2]
    quarter = d_model // 4
    bf16, dma = jnp.bfloat16, pltpu.SemaphoreType.DMA
    outs = pl.pallas_call(
        layer_kernel,
        name='moe_layer',
        out_shape=[jax.ShapeDtypeStruct((n_ep, 4, n_rows, quarter), bf16),
                   jax.ShapeDtypeStruct((n_ep - 1, n_rows, d_model), bf16),
                   jax.ShapeDtypeStruct((3, d_model, ff), bf16),
                   jax.ShapeDtypeStruct((3, d_model, ff), bf16),
                   jax.ShapeDtypeStruct((3, ff, d_model), bf16)],
        in_specs=[ANY] * 4,
        out_specs=[ANY] * 5,
        scratch_shapes=[pltpu.VMEM((2, n_rows, d_model), bf16),
                        pltpu.VMEM((2, d_model, ff), bf16),
                        pltpu.VMEM((2, d_model, ff), bf16),
                        pltpu.VMEM((2, ff, d_model), bf16),
                        pltpu.VMEM((n_rows, ff), bf16),
                        pltpu.VMEM((4, n_rows, quarter), jnp.float32),
                        pltpu.VMEM((n_ep, 4, n_rows, quarter), bf16),
                        dma((2,)), dma((2, 3)), dma,
                        dma((n_ep - 1,)), dma((n_ep - 1,)), dma((3,)), dma((3,)),
                        dma((6,)), dma((6,)), dma((6,)), dma((6,)),
                        dma((6,)), dma((6,)), dma((6,)), dma((6,)),
                        dma((n_ep, 4)), dma((n_ep, 4))],
        compiler_params=pltpu.CompilerParams(has_side_effects=True, vmem_limit_bytes=VMEM_LIMIT),
    )(rows, wg, wu, wd)
    return outs[0]


def combine_kernel(first, second, gate0, gate1, results, out, wide, tile):
    n_res = results.shape[0]
    tokens = out.shape[0]
    block = n_res // 16

    def widen(r, carry):
        at = pl.ds(pl.multiple_of(r * block, 8), block)
        wide[at, :] = results[at, :].astype(jnp.float32)
        return carry

    lax.fori_loop(0, 16, widen, 0)
    wide[pl.ds(n_res, 8), :] = jnp.zeros((8, wide.shape[1]), jnp.float32)
    chunk = tile.shape[0]

    def chunk_body(b, carry):
        def eight(i, carry):
            for u in range(8):
                local = i * 8 + u
                t = b * chunk + local
                row = gate0[t] * wide[pl.ds(first[t], 1), :] + gate1[t] * wide[pl.ds(second[t], 1), :]
                tile[pl.ds(local, 1), :] = row
            return carry

        lax.fori_loop(0, chunk // 8, eight, 0)
        out[pl.ds(pl.multiple_of(b * chunk, 8), chunk), :] = tile[...].astype(jnp.bfloat16)
        return carry

    lax.fori_loop(0, tokens // chunk, chunk_body, 0)


def run_combine(index, gates, results):
    tokens = index.shape[1]
    cols = results.shape[1]
    smem = pl.BlockSpec(memory_space=pltpu.SMEM)
    vmem = pl.BlockSpec(memory_space=pltpu.VMEM)
    return pl.pallas_call(
        combine_kernel,
        name='moe_combine',
        out_shape=jax.ShapeDtypeStruct((tokens, cols), jnp.bfloat16),
        in_specs=[smem] * 4 + [vmem],
        out_specs=vmem,
        scratch_shapes=[pltpu.VMEM((results.shape[0] + 8, cols), jnp.float32),
                        pltpu.VMEM((min(256, tokens), cols), jnp.float32)],
        compiler_params=pltpu.CompilerParams(vmem_limit_bytes=VMEM_LIMIT),
    )(index[0], index[1], gates[0], gates[1], results)


def solution(mesh):
    n_ep = mesh.shape['ep']
    row_spec = P(('dp', 'ep'), None)

    def device_body(x_loc, ids_loc, gates_loc, wg_loc, wu_loc, wd_loc):
        tokens, d_model = x_loc.shape
        n_top = ids_loc.shape[1]
        local_experts = wg_loc.shape[0]
        n_experts = local_experts * n_ep
        capacity = CAP_NUM * n_top * tokens // (CAP_DEN * n_experts)
        half = capacity // 2
        tp = lax.axis_index('tp')
        parity, part = tp // 2, tp % 2
        chosen, slots = slot_numbers(ids_loc, n_experts)
        taken = jnp.where(chosen, slots, -1).reshape(n_ep, local_experts, tokens)
        taken = lax.dynamic_index_in_dim(taken, parity, axis=1, keepdims=False)
        wanted = part * half + jnp.arange(half, dtype=jnp.int32)
        number = jnp.arange(tokens, dtype=jnp.int32)
        owner = jnp.max(jnp.where(taken[:, None, :] == wanted[None, :, None], number, 0), axis=2)
        rows = jnp.take(x_loc, owner, axis=0, mode='clip')
        ids_t = ids_loc.T
        expert = jnp.arange(n_experts, dtype=jnp.int32)[None, :, None]
        copy_slot = jnp.sum(jnp.where(ids_t[:, None, :] == expert, slots[None], 0), axis=1)
        index = jnp.where(copy_slot < capacity, ids_t * capacity + copy_slot, n_experts * capacity)
        results = run_layer(rows, wg_loc, wu_loc, wd_loc)
        results = results.reshape(n_experts * capacity, d_model // 4)
        mine = run_combine(index, gates_loc.T, results)
        return lax.all_gather(mine, 'tp', axis=1, tiled=True)

    return jax.shard_map(device_body, mesh=mesh,
                         in_specs=(row_spec, row_spec, row_spec, P('ep', None, 'tp'), P('ep', None, 'tp'), P('ep', 'tp', None)),
                         out_specs=row_spec, check_vma=False)
```

time: 2250 us -> 736 us (0.33)
  blocking collectives: 945 us -> 0 us
  Pallas kernels: 0 us -> 560 us
  waiting for transfers between devices: 499 us -> 107 us
  local copies, waits for them, and re-layouts: 370 us -> 45.6 us
  matrix products: 225 us -> 0.29 us
  other arithmetic: 183 us -> 8.85 us
    all_to_all x3 -> x0, blocking collectives: 945 us -> none  [the longest x1 474 us: device_body(): pieces = lax.all_to_all(part_out, 'tp', 1, 1, tiled=True)]
    pallas_call x0 -> x2, Pallas kernels: none -> 560 us  [the longest x1 526 us: run_layer(): pl.pallas_call(layer_kernel, name='moe_layer', out_shape=[jax.ShapeDtypeS...]
    all_gather x2 -> x1, waiting for transfers between devices: 499 us -> 107 us  [device_body(): return lax.all_gather(mine, 'tp', axis=1, tiled=True)]
    gather x3 -> x1, local copies, waits for them, and re-layouts: 272 us -> 28.3 us  [device_body(): rows = jnp.take(x_loc, owner, axis=0, mode='clip')]
    dot_general x3 -> x2, matrix products: 225 us -> 0.29 us  [the longest x1 0.17 us: slot_numbers(): jnp.einsum('ebi,ij->ebj', bits, before, preferred_element_type=jnp.float32)]
    reduce_sum x3 -> x2, other arithmetic: 169 us -> 0.98 us  [the longest x1 0.87 us: device_body(): jnp.sum(jnp.where(ids_t[:, None, :] == expert, slots[None], 0), axis=1)]
    reshape x4 -> x1, local copies, waits for them, and re-layouts: 41 us -> 0.07 us  [slot_numbers(): (inside + offsets[:, :, None]).astype(jnp.int32).reshape(n_experts, tokens)]
    scatter x1 -> x0, local copies, waits for them, and re-layouts: 30.9 us -> none  [local_routing(): jnp.full((n_experts * capacity + 1,), tokens, jnp.int32).at[flat_slot]]
  transfers between devices with their start and end apart: 2 -> 1, of which waited for: 2 -> 1; matrix products, arithmetic and copies ran while one was open for 0% -> 0% of each run, Pallas kernels for 0% -> 0%
where the time goes in v1:
time: 736 us; the launch traced here: 735 us
  Pallas kernels  560 us (76%)
  waiting for transfers between devices  107 us (15%)
  local copies, waits for them, and re-layouts  45.6 us (6%)
  between operations  13.4 us (2%)
  other arithmetic  8.85 us (1%)
    pallas_call x1, Pallas kernels, run_layer(): pl.pallas_call(layer_kernel, name='moe_layer', out_shape=[jax.ShapeDtypeS...  526 us
    all_gather x1, waiting for transfers between devices, device_body(): return lax.all_gather(mine, 'tp', axis=1, tiled=True)  107 us
    pallas_call x1, Pallas kernels, run_combine(): pl.pallas_call(combine_kernel, name='moe_combine', out_shape=jax.ShapeDty...  33.8 us
    gather x1, local copies, waits for them, and re-layouts, device_body(): rows = jnp.take(x_loc, owner, axis=0, mode='clip')  28.3 us
  transfers between devices with their start and end apart: 1, of which 1 were waited for; matrix products, arithmetic and copies ran while one was open for 0% of the time, Pallas kernels for 0%

profile of v1, /device:TPU:0, one launch (start us, length us, event | category | flops | bytes accessed | tf_op | source)
XLA Modules:
  0.0 735.4 jit_solution(16229202333040065917)
XLA Ops:
  6.5 0.0 all-gather.2.cloned.1.call-start
  6.5 1.5 fusion.10
  8.0 0.9 fusion.12
  8.9 0.1 fusion.4
  9.0 0.1 fusion.9
  9.1 0.2 fusion
  9.3 0.1 reshape.56
  9.4 0.1 copy.11
  9.5 0.9 select_reduce_fusion.1
  10.3 0.8 compare_select_fusion
  11.1 0.6 fusion.11
  11.7 0.1 constant_dynamic-slice_fusion
  11.8 0.2 or_select_fusion
  12.0 6.9 select_reduce_fusion
  19.0 28.3 %gather_fusion = bf16[2560,2048]{1,0:T(8,128)(2,1)} fusion(bf16[4096,2048]{1,0:T(8,128)(2,1)} %param.6, s32[3072]{0:T(1024)S(1)} %pad_clamp_fusion), kind=kCustom, calls=%fused_computation | custom fusion | bytes 20981760 | tf_op jit(solution)/shard_map/jit(_take)/gather | solution.py:349
  47.2 526.2 %moe_layer.1 = (bf16[4,4,640,512]{3,2,1,0:T(8,128)(2,1)}, bf16[3,640,2048]{2,1,0:T(8,128)(2,1)}, bf16[3,2048,1408]{2,1,0:T(8,128)(2,1)}, bf16[3,2048,1408]{2,1,0:T(8,128)(2,1)}, bf16[3,1408,2048]{2,1,0:T(8,128)(2,1)}) custom-call(bf16[4,640,2048]{2,1,0:T(8,128)(2,1)} %bitcast.24, bf16[2,2048,1408]{2,1,0:T(8,128)(2,1)} %wg.1, bf16[2,2048,1408]{2,1,0:T(8,128)(2,1)} %wu.1, ...), custom_call_target="tpu_custom_call" | custom-call | tf_op jit(solution)/shard_map/moe_layer/pallas_call | solution.py:256
  573.4 33.8 %moe_combine.1 = bf16[4096,512]{1,0:T(8,128)(2,1)} custom-call(s32[4096]{0:T(1024)} %bitcast.38, s32[4096]{0:T(1024)} %bitcast.37, f32[4096]{0:T(1024)} %bitcast.36, f32[4096]{0:T(1024)} %bitcast.35, bf16[10240,512]{1,0:T(8,128)(2,1)} %bitcast.25), custom_call_target="tpu_custom_call" | custom-call | tf_op jit(solution)/shard_map/moe_combine/pallas_call | solution.py:318
  607.2 0.0 all-gather.2.cloned.1.call-update
  607.2 107.2 %all-gather.2.cloned.1.call-done = bf16[4096,2048]{1,0:T(8,128)(2,1)} async-done(((bf16[4096,512]{1,0:T(8,128)(2,1)}), bf16[4096,2048]{1,0:T(8,128)(2,1)}) %all-gather.2.cloned.1.call-update) | async-done | bytes 16777232 | tf_op jit(solution)/shard_map/all_gather | solution.py:357
  714.4 14.2 %copy.14 = bf16[4096,2048]{1,0:T(8,128)(2,1)} copy(bf16[4096,2048]{1,0:T(8,128)(2,1)} %all-gather.2.cloned.1.call-done) | data formatting | bytes 33554432
  (5 shorter events, 0.1 us)
Async XLA Ops:
  6.5 707.9 %all-gather.2.cloned.1.call-start = ((), (), s32[]{:S(2)}) async-start(), calls=%async_computation | async-start | bytes 20971520 | tf_op jit(solution)/shard_map/all_gather | solution.py:357
Sparse Core Ops, SparseCore 0:
  607.3 107.0 all-gather.1

commit v2 on v1

--- a/solution.py
+++ b/solution.py
@@ -8,6 +8,9 @@
 CAP_NUM = 5
 CAP_DEN = 4
 MESH = pl.DeviceIdType.MESH
+SUBS = 4
+PIECES = 3 * SUBS
+AHEAD = 2
 ANY = pl.BlockSpec(memory_space=pl.ANY)
 VMEM_LIMIT = 67_043_328
 
@@ -54,26 +57,26 @@
     peer_core = (dp, z, 2 * y + 1 - c)
 
     def piece(p, half):
-        size = w_in[p // 2].shape[1] // 4
-        return pl.ds(pl.multiple_of(half * 2 * size + (p % 2) * size, 16), size)
+        size = w_in[p // SUBS].shape[1] // (2 * SUBS)
+        return pl.ds(pl.multiple_of((half * SUBS + p % SUBS) * size, 16), size)
 
     def core_copy(a):
         return remote(w_in[a].at[y], w_buf[a].at[0], core_s.at[a], core_r.at[a], peer_core)
 
     def y_copy(p):
-        a, at = p // 2, piece(p, dp)
+        a, at = p // SUBS, piece(p, dp)
         return remote(w_in[a].at[1 - y, at], w_buf[a].at[1, at], y_s.at[p], y_r.at[p], (dp, z, 2 * (1 - y) + c))
 
     def x_copy(p):
-        a, at = p // 2, piece(p, dp)
+        a, at = p // SUBS, piece(p, dp)
         return remote(w_buf[a].at[1, at], w_buf[a].at[1, at], x_s.at[p], x_r.at[p], (1 - dp, z, tp))
 
     def d1_copy(p):
-        a, at = p // 2, piece(p, dp)
+        a, at = p // SUBS, piece(p, dp)
         return remote(w_buf[a].at[1, at], w_buf[a].at[2, at], d1_s.at[p], d1_r.at[p], peer_core)
 
     def d2_copy(p):
-        a, at = p // 2, piece(p, 1 - dp)
+        a, at = p // SUBS, piece(p, 1 - dp)
         return remote(w_buf[a].at[1, at], w_buf[a].at[2, at], d2_s.at[p], d2_r.at[p], peer_core)
 
     def dispatch(k):
@@ -91,6 +94,9 @@
         y_copy(p).wait_recv()
         x_copy(p).start()
         d1_copy(p).start()
+        if p + AHEAD < PIECES:
+            y_copy(p).wait_send()
+            y_copy(p + AHEAD).start()
 
     def forward_x(p):
         x_copy(p).wait_recv()
@@ -110,19 +116,19 @@
     def load_x(src, slot):
         return pltpu.make_async_copy(src, xv.at[slot], x_sem.at[slot])
 
-    for k in range(n_ep - 1):
-        dispatch(k).start()
+    dispatch(0).start()
+    for p in range(AHEAD):
+        y_copy(p).start()
     for a in range(3):
         core_copy(a).start()
+    start_w(0, 0)
     for p in range(6):
-        y_copy(p).start()
-    start_w(0, 0)
-    forward_y(0)
-    forward_y(1)
-    forward_x(0)
-    forward_y(2)
-    forward_x(1)
+        forward_y(p)
+        if p >= 2:
+            forward_x(p - 2)
     dispatch(0).wait_recv()
+    for k in range(1, n_ep - 1):
+        dispatch(k).start()
     load_x(arrived.at[0], 0).start()
 
     def step_body(step, carry):
@@ -137,7 +143,7 @@
 
         @pl.when(step == 2)
         def _():
-            for p in range(6):
+            for p in range(PIECES):
                 d1_copy(p).wait_recv()
                 d2_copy(p).wait_recv()
 
@@ -201,16 +207,17 @@
 
         @pl.when(step == 0)
         def _():
-            forward_y(3)
-            forward_x(2)
+            for p in range(6, 8):
+                forward_y(p)
+                forward_x(p - 2)
 
         @pl.when(step == 1)
         def _():
-            forward_y(4)
-            forward_x(3)
-            forward_y(5)
-            forward_x(4)
-            forward_x(5)
+            for p in range(8, PIECES):
+                forward_y(p)
+                forward_x(p - 2)
+            for p in range(PIECES - 2, PIECES):
+                forward_x(p)
             start_w(2, 1 - slot)
 
         @pl.when((j == 3) & (k < n_ep - 1))
@@ -228,8 +235,9 @@
         dispatch(k).wait_send()
     for a in range(3):
         core_copy(a).wait_send()
-    for p in range(6):
-        y_copy(p).wait_send()
+    for p in range(PIECES):
+        if p + AHEAD >= PIECES:
+            y_copy(p).wait_send()
         x_copy(p).wait_send()
         d1_copy(p).wait_send()
         d2_copy(p).wait_send()
@@ -272,17 +280,43 @@
                         pltpu.VMEM((n_ep, 4, n_rows, quarter), bf16),
                         dma((2,)), dma((2, 3)), dma,
                         dma((n_ep - 1,)), dma((n_ep - 1,)), dma((3,)), dma((3,)),
-                        dma((6,)), dma((6,)), dma((6,)), dma((6,)),
-                        dma((6,)), dma((6,)), dma((6,)), dma((6,)),
+                        *[dma((PIECES,)) for _ in range(8)],
                         dma((n_ep, 4)), dma((n_ep, 4))],
         compiler_params=pltpu.CompilerParams(has_side_effects=True, vmem_limit_bytes=VMEM_LIMIT),
     )(rows, wg, wu, wd)
     return outs[0]
 
 
-def combine_kernel(first, second, gate0, gate1, results, out, wide, tile):
-    n_res = results.shape[0]
-    tokens = out.shape[0]
+CHUNKS = 8
+
+
+def combine_kernel(first, second, gate0, gate1, results, out, wide, tile, done,
+                   own_s, core_s, core_r, y_s, y_r, fwd_s, fwd_r):
+    dp, z, tp = lax.axis_index('dp'), lax.axis_index('ep'), lax.axis_index('tp')
+    y, c = tp // 2, tp % 2
+    n_res, cols = results.shape
+    chunk = done.shape[1]
+    peer_core, peer_chip = 2 * y + 1 - c, 2 * (1 - y) + c
+
+    def place(b, quarter):
+        return out.at[pl.ds(pl.multiple_of(b * chunk, 16), chunk), pl.ds(pl.multiple_of(quarter * cols, 128), cols)]
+
+    def remote(src, dst, send, recv, device):
+        return pltpu.make_async_remote_copy(src_ref=src, dst_ref=dst, send_sem=send, recv_sem=recv,
+                                            device_id=(dp, z, device), device_id_type=MESH)
+
+    def own(b):
+        return pltpu.make_async_copy(done.at[b], place(b, tp), own_s.at[b])
+
+    def to_core(b):
+        return remote(done.at[b], place(b, tp), core_s.at[b], core_r.at[b], peer_core)
+
+    def to_chip(b):
+        return remote(done.at[b], place(b, tp), y_s.at[b], y_r.at[b], peer_chip)
+
+    def forward(b):
+        return remote(place(b, peer_chip), place(b, peer_chip), fwd_s.at[b], fwd_r.at[b], peer_core)
+
     block = n_res // 16
 
     def widen(r, carry):
@@ -291,39 +325,61 @@
         return carry
 
     lax.fori_loop(0, 16, widen, 0)
-    wide[pl.ds(n_res, 8), :] = jnp.zeros((8, wide.shape[1]), jnp.float32)
-    chunk = tile.shape[0]
-
-    def chunk_body(b, carry):
-        def eight(i, carry):
+    wide[pl.ds(n_res, 8), :] = jnp.zeros((8, cols), jnp.float32)
+    part = tile.shape[0]
+
+    def part_body(i, carry):
+        def eight(g, carry):
             for u in range(8):
-                local = i * 8 + u
-                t = b * chunk + local
+                local = g * 8 + u
+                t = i * part + local
                 row = gate0[t] * wide[pl.ds(first[t], 1), :] + gate1[t] * wide[pl.ds(second[t], 1), :]
                 tile[pl.ds(local, 1), :] = row
             return carry
 
-        lax.fori_loop(0, chunk // 8, eight, 0)
-        out[pl.ds(pl.multiple_of(b * chunk, 8), chunk), :] = tile[...].astype(jnp.bfloat16)
+        lax.fori_loop(0, part // 8, eight, 0)
+        per = chunk // part
+        b = i // per
+        done[b, pl.ds(pl.multiple_of(i % per * part, 16), part), :] = tile[...].astype(jnp.bfloat16)
+
+        @pl.when(i % per == per - 1)
+        def _():
+            to_chip(b).start()
+            to_core(b).start()
+            own(b).start()
         return carry
 
-    lax.fori_loop(0, tokens // chunk, chunk_body, 0)
+    lax.fori_loop(0, CHUNKS * chunk // part, part_body, 0)
+    for b in range(CHUNKS):
+        to_chip(b).wait_recv()
+        forward(b).start()
+    for b in range(CHUNKS):
+        own(b).wait()
+        to_chip(b).wait_send()
+        to_core(b).wait_send()
+        forward(b).wait_send()
+        to_core(b).wait_recv()
+        forward(b).wait_recv()
 
 
 def run_combine(index, gates, results):
     tokens = index.shape[1]
     cols = results.shape[1]
+    chunk = tokens // CHUNKS
+    bf16, dma = jnp.bfloat16, pltpu.SemaphoreType.DMA
     smem = pl.BlockSpec(memory_space=pltpu.SMEM)
     vmem = pl.BlockSpec(memory_space=pltpu.VMEM)
     return pl.pallas_call(
         combine_kernel,
         name='moe_combine',
-        out_shape=jax.ShapeDtypeStruct((tokens, cols), jnp.bfloat16),
+        out_shape=jax.ShapeDtypeStruct((tokens, 4 * cols), bf16),
         in_specs=[smem] * 4 + [vmem],
-        out_specs=vmem,
+        out_specs=ANY,
         scratch_shapes=[pltpu.VMEM((results.shape[0] + 8, cols), jnp.float32),
-                        pltpu.VMEM((min(256, tokens), cols), jnp.float32)],
-        compiler_params=pltpu.CompilerParams(vmem_limit_bytes=VMEM_LIMIT),
+                        pltpu.VMEM((min(256, chunk), cols), jnp.float32),
+                        pltpu.VMEM((CHUNKS, chunk, cols), bf16),
+                        *[dma((CHUNKS,)) for _ in range(7)]],
+        compiler_params=pltpu.CompilerParams(has_side_effects=True, vmem_limit_bytes=VMEM_LIMIT),
     )(index[0], index[1], gates[0], gates[1], results)
 
 
@@ -353,8 +409,7 @@
         index = jnp.where(copy_slot < capacity, ids_t * capacity + copy_slot, n_experts * capacity)
         results = run_layer(rows, wg_loc, wu_loc, wd_loc)
         results = results.reshape(n_experts * capacity, d_model // 4)
-        mine = run_combine(index, gates_loc.T, results)
-        return lax.all_gather(mine, 'tp', axis=1, tiled=True)
+        return run_combine(index, gates_loc.T, results)
 
     return jax.shard_map(device_body, mesh=mesh,
                          in_specs=(row_spec, row_spec, row_spec, P('ep', None, 'tp'), P('ep', None, 'tp'), P('ep', 'tp', None)),

time: 736 us -> 657 us (0.89)
  waiting for transfers between devices: 107 us -> 0 us
  Pallas kernels: 560 us -> 602 us
  between operations: 13.4 us -> 0.07 us
    all_gather x1 -> x0, waiting for transfers between devices: 107 us -> none  [device_body(): return lax.all_gather(mine, 'tp', axis=1, tiled=True)]
    pallas_call x1, Pallas kernels: 33.8 us -> 108 us  [run_combine(): pl.pallas_call(combine_kernel, name='moe_combine', out_shape=jax.ShapeDty...]
    pallas_call x1, Pallas kernels: 526 us -> 494 us  [run_layer(): pl.pallas_call(layer_kernel, name='moe_layer', out_shape=[jax.ShapeDtypeS...]
  transfers between devices with their start and end apart: 1 -> 0, of which waited for: 1 -> 0; matrix products, arithmetic and copies ran while one was open for 0% -> 0% of each run, Pallas kernels for 0% -> 0%
where the time goes in v2:
time: 657 us
  Pallas kernels  602 us (92%)
  local copies, waits for them, and re-layouts  45.6 us (7%)
  other arithmetic  8.85 us (1%)
    pallas_call x1, Pallas kernels, run_layer(): pl.pallas_call(layer_kernel, name='moe_layer', out_shape=[jax.ShapeDtypeS...  494 us
    pallas_call x1, Pallas kernels, run_combine(): pl.pallas_call(combine_kernel, name='moe_combine', out_shape=jax.ShapeDty...  108 us
    gather x1, local copies, waits for them, and re-layouts, device_body(): rows = jnp.take(x_loc, owner, axis=0, mode='clip')  28.3 us
    unnamed x3, local copies, waits for them, and re-layouts  14.3 us

profile of v2, /device:TPU:0, one launch (start us, length us, event | category | flops | bytes accessed | tf_op | source)
XLA Modules:
  0.0 656.8 jit_solution(9235576885283186164)
XLA Ops:
  0.0 0.1 constant_dynamic-slice_fusion
  0.1 1.5 fusion.10
  1.5 0.9 fusion.12
  2.4 0.1 fusion.4
  2.5 0.1 fusion.9
  2.7 0.2 fusion
  2.8 0.1 copy.11
  2.9 0.9 select_reduce_fusion.1
  3.8 0.8 compare_select_fusion
  4.6 0.6 fusion.11
  5.2 0.1 reshape.56
  5.3 0.2 or_select_fusion
  5.5 6.9 %select_reduce_fusion = s32[4,640]{1,0:T(4,128)S(1)} fusion(s32[4,4096]{1,0:T(4,128)S(1)} %bitcast.35, s32[640]{0:T(1024)S(1)} %iota_add_fusion), kind=kLoop, calls=%fused_computation.1 | loop fusion | flops 31454720 | bytes 78336 | tf_op jit(solution)/shard_map/reduce_max | solution.py:404
  12.4 28.3 %gather_fusion = bf16[2560,2048]{1,0:T(8,128)(2,1)} fusion(bf16[4096,2048]{1,0:T(8,128)(2,1)} %param.6, s32[3072]{0:T(1024)S(1)} %pad_clamp_fusion), kind=kCustom, calls=%fused_computation | custom fusion | bytes 20981760 | tf_op jit(solution)/shard_map/jit(_take)/gather | solution.py:405
  40.7 494.0 %moe_layer.1 = (bf16[4,4,640,512]{3,2,1,0:T(8,128)(2,1)}, bf16[3,640,2048]{2,1,0:T(8,128)(2,1)}, bf16[3,2048,1408]{2,1,0:T(8,128)(2,1)}, bf16[3,2048,1408]{2,1,0:T(8,128)(2,1)}, bf16[3,1408,2048]{2,1,0:T(8,128)(2,1)}) custom-call(bf16[4,640,2048]{2,1,0:T(8,128)(2,1)} %bitcast.24, bf16[2,2048,1408]{2,1,0:T(8,128)(2,1)} %wg.1, bf16[2,2048,1408]{2,1,0:T(8,128)(2,1)} %wu.1, ...), custom_call_target="tpu_custom_call" | custom-call | tf_op jit(solution)/shard_map/moe_layer/pallas_call | solution.py:264
  534.6 107.9 %moe_combine.1 = bf16[4096,2048]{1,0:T(8,128)(2,1)} custom-call(s32[4096]{0:T(1024)} %bitcast.39, s32[4096]{0:T(1024)} %bitcast.38, f32[4096]{0:T(1024)} %bitcast.37, f32[4096]{0:T(1024)} %bitcast.36, bf16[10240,512]{1,0:T(8,128)(2,1)} %bitcast.25), custom_call_target="tpu_custom_call" | custom-call | tf_op jit(solution)/shard_map/moe_combine/pallas_call | solution.py:372
  642.6 14.2 %copy.14 = bf16[4096,2048]{1,0:T(8,128)(2,1)} copy(bf16[4096,2048]{1,0:T(8,128)(2,1)} %moe_combine.1) | data formatting | bytes 33554432
  (5 shorter events, 0.1 us)

commit v3 on v2

--- a/solution.py
+++ b/solution.py
@@ -35,10 +35,10 @@
     return bit + mask - 2 * bit * mask
 
 
-def layer_kernel(rows, wg, wu, wd, ret, arrived, bg, bu, bd,
+def layer_kernel(taken, x, wg, wu, wd, ret, rows, arrived, bg, bu, bd,
                  xv, gv, uv, dv, hv, acc, yv,
-                 x_sem, w_sem, own_sem,
-                 disp_s, disp_r, core_s, core_r, y_s, y_r, x_s, x_r, d1_s, d1_r, d2_s, d2_r, ret_s, ret_r):
+                 x_sem, w_sem, own_sem, row_sem,
+                 first_s, first_r, disp_s, disp_r, core_s, core_r, y_s, y_r, x_s, x_r, d1_s, d1_r, d2_s, d2_r, ret_s, ret_r):
     dp, z, tp = lax.axis_index('dp'), lax.axis_index('ep'), lax.axis_index('tp')
     y, c = tp // 2, tp % 2
     n_rows = rows.shape[1]
@@ -80,7 +80,11 @@
         return remote(w_buf[a].at[1, at], w_buf[a].at[2, at], d2_s.at[p], d2_r.at[p], peer_core)
 
     def dispatch(k):
-        return remote(rows.at[partner(k)], arrived.at[k], disp_s.at[k], disp_r.at[k], (dp, partner(k), tp))
+        return remote(rows.at[k], arrived.at[k], disp_s.at[k], disp_r.at[k], (dp, partner(k), tp))
+
+    def dispatch_first(q):
+        cols = pl.ds(pl.multiple_of(q * ret.shape[3], 128), ret.shape[3])
+        return remote(rows.at[0, :, cols], arrived.at[0, :, cols], first_s.at[q], first_r.at[q], (dp, partner(0), tp))
 
     def give_back(k, step):
         quarter = (tp + step) % n_tp
@@ -116,20 +120,117 @@
     def load_x(src, slot):
         return pltpu.make_async_copy(src, xv.at[slot], x_sem.at[slot])
 
-    dispatch(0).start()
     for p in range(AHEAD):
         y_copy(p).start()
     for a in range(3):
         core_copy(a).start()
+
+    tokens, d_model = x.shape
+    half_t, half_d = tokens // 2, d_model // 2
+    quarter_cols = ret.shape[3]
+
+    def load_tokens(h, side):
+        return pltpu.make_async_copy(x.at[pl.ds(h * half_t, half_t), pl.ds(side * half_d, half_d)],
+                                     w_vmem[h].at[side, pl.ds(0, half_t), pl.ds(0, half_d)], w_sem.at[side, h])
+
+    def store_rows(k, q):
+        cols = pl.ds(pl.multiple_of(q * quarter_cols, 128), quarter_cols)
+        return pltpu.make_async_copy(yv.at[k, q], rows.at[k, :, cols], row_sem.at[q])
+
+    for side in range(2):
+        for h in range(2):
+            load_tokens(h, side).start()
+
+    def pick_rows(k, carry):
+        wanted = lax.broadcasted_iota(jnp.int32, (n_rows, 128), 0) + c * n_rows
+        for h in range(2):
+            def mark(t, carry):
+                at = pl.multiple_of(t * 128, 128)
+                owned = taken.at[partner(k)][pl.ds(h * (half_t // 128) + t, 1), :]
+                xv.at[h][:, pl.ds(at, 128)] = jnp.where(owned == wanted, 1.0, 0.0).astype(jnp.bfloat16)
+                return carry
+
+            lax.fori_loop(0, half_t // 128, mark, 0)
+
+        @pl.when(k == 0)
+        def _():
+            for side in range(2):
+                for h in range(2):
+                    load_tokens(h, side).wait()
+
+        def pick_cols(q, carry):
+            at = pl.ds(pl.multiple_of(q % 2 * quarter_cols, 128), quarter_cols)
+            picked = [jnp.dot(xv.at[h][:, pl.ds(0, half_t)], w_vmem[h].at[q // 2][pl.ds(0, half_t), at],
+                              preferred_element_type=jnp.float32) for h in range(2)]
+            yv.at[k, q][...] = (picked[0] + picked[1]).astype(jnp.bfloat16)
+            store_rows(k, q).start()
+
+            @pl.when(k == 0)
+            def _():
+                store_rows(k, q).wait()
+                dispatch_first(q).start()
+            return carry
+
+        lax.fori_loop(0, n_tp, pick_cols, 0)
+
+        @pl.when(k > 0)
+        def _():
+            for q in range(n_tp):
+                store_rows(k, q).wait()
+
+        @pl.when(k == 2)
+        def _():
+            for p in range(2):
+                forward_y(p)
+        return carry
+
+    lax.fori_loop(0, n_ep, pick_rows, 0)
     start_w(0, 0)
-    for p in range(6):
+    for p in range(2, 6):
         forward_y(p)
-        if p >= 2:
-            forward_x(p - 2)
-    dispatch(0).wait_recv()
+        forward_x(p - 2)
+    for q in range(n_tp):
+        dispatch_first(q).wait_recv()
     for k in range(1, n_ep - 1):
         dispatch(k).start()
     load_x(arrived.at[0], 0).start()
+
+    def gate_up_all(x_slot, slot, h_slot):
+        def gate_up(at):
+            x_now = xv.at[x_slot][...]
+            gate = jnp.dot(x_now, gv.at[slot][:, at], preferred_element_type=jnp.float32)
+            up = jnp.dot(x_now, uv.at[slot][:, at], preferred_element_type=jnp.float32)
+            hv.at[h_slot][:, at] = (jax.nn.silu(gate) * up).astype(jnp.bfloat16)
+
+        wide = 256
+
+        def gate_up_loop(t, carry):
+            gate_up(pl.ds(pl.multiple_of(t * wide, 128), wide))
+            return carry
+
+        lax.fori_loop(0, ff // wide, gate_up_loop, 0)
+        if ff % wide:
+            gate_up(pl.ds(ff // wide * wide, ff % wide))
+
+    def down_all(k, j, slot, h_slot):
+        def down_loop(q, carry):
+            at = pl.ds(pl.multiple_of(q * quarter_cols, 128), quarter_cols)
+            part = jnp.dot(hv.at[h_slot][...], dv.at[slot][:, at], preferred_element_type=jnp.float32)
+
+            @pl.when(j == 0)
+            def _():
+                acc.at[q][...] = part
+
+            @pl.when((j > 0) & (j < 3))
+            def _():
+                acc.at[q][...] += part
+
+            @pl.when(j == 3)
+            def _():
+                yv.at[k, q][...] = (acc.at[q][...] + part).astype(jnp.bfloat16)
+            return carry
+
+        lax.fori_loop(0, n_tp, down_loop, 0)
 
     def step_body(step, carry):
         k, j = step // 4, step % 4
@@ -141,12 +242,6 @@
             for a in range(3):
                 core_copy(a).wait_recv()
 
-        @pl.when(step == 2)
-        def _():
-            for p in range(PIECES):
-                d1_copy(p).wait_recv()
-                d2_copy(p).wait_recv()
-
         @pl.when((step != 1) & (step < last))
         def _():
             start_w((j + 1) % 4, 1 - slot)
@@ -162,48 +257,13 @@
 
         @pl.when((j == 3) & (k == n_ep - 2))
         def _():
-            load_x(rows.at[z], 1 - x_slot).start()
+            load_x(rows.at[n_ep - 1], 1 - x_slot).start()
 
         for a in range(2):
             load_w(0, slot, a).wait()
-
-        def gate_up(at):
-            x_now = xv.at[x_slot][...]
-            gate = jnp.dot(x_now, gv.at[slot][:, at], preferred_element_type=jnp.float32)
-            up = jnp.dot(x_now, uv.at[slot][:, at], preferred_element_type=jnp.float32)
-            hv[:, at] = (jax.nn.silu(gate) * up).astype(jnp.bfloat16)
-
-        wide = 256
-
-        def gate_up_loop(t, carry):
-            gate_up(pl.ds(pl.multiple_of(t * wide, 128), wide))
-            return carry
-
-        lax.fori_loop(0, ff // wide, gate_up_loop, 0)
-        if ff % wide:
-            gate_up(pl.ds(ff // wide * wide, ff % wide))
-
+        gate_up_all(x_slot, slot, 0)
         load_w(0, slot, 2).wait()
-        quarter_cols = ret.shape[3]
-
-        def down_loop(q, carry):
-            at = pl.ds(pl.multiple_of(q * quarter_cols, 128), quarter_cols)
-            part = jnp.dot(hv[...], dv.at[slot][:, at], preferred_element_type=jnp.float32)
-
-            @pl.when(j == 0)
-            def _():
-                acc.at[q][...] = part
-
-            @pl.when((j > 0) & (j < 3))
-            def _():
-                acc.at[q][...] += part
-
-            @pl.when(j == 3)
-            def _():
-                yv.at[k, q][...] = (acc.at[q][...] + part).astype(jnp.bfloat16)
-            return carry
-
-        lax.fori_loop(0, n_tp, down_loop, 0)
+        down_all(k, j, slot, 0)
 
         @pl.when(step == 0)
         def _():
@@ -211,27 +271,59 @@
                 forward_y(p)
                 forward_x(p - 2)
 
-        @pl.when(step == 1)
-        def _():
-            for p in range(8, PIECES):
-                forward_y(p)
-                forward_x(p - 2)
-            for p in range(PIECES - 2, PIECES):
-                forward_x(p)
-            start_w(2, 1 - slot)
-
         @pl.when((j == 3) & (k < n_ep - 1))
         def _():
             for q in range(n_tp):
                 give_back(k, q).start()
         return carry
 
-    lax.fori_loop(0, 4 * n_ep, step_body, 0)
+    lax.fori_loop(0, 2, step_body, 0)
+    gates_done = 2 * SUBS
+    for p in range(gates_done, gates_done + 2):
+        forward_y(p)
+        forward_x(p - 2)
+    for a in range(2):
+        load_w(2, 0, a).start()
+    for p in range(gates_done):
+        d1_copy(p).wait_recv()
+        d2_copy(p).wait_recv()
+    for a in range(2):
+        load_w(3, 1, a).start()
+    for a in range(2):
+        load_w(2, 0, a).wait()
+    gate_up_all(0, 0, 0)
+    forward_y(gates_done + 2)
+    forward_x(gates_done)
+    for a in range(2):
+        load_w(3, 1, a).wait()
+    gate_up_all(0, 1, 1)
+    for a in range(2):
+        load_w(0, 0, a).start()
+    forward_y(gates_done + 3)
+    for p in range(gates_done + 1, PIECES):
+        forward_x(p)
+    load_w(2, 0, 2).start()
+    for p in range(gates_done, PIECES):
+        d1_copy(p).wait_recv()
+        d2_copy(p).wait_recv()
+    load_w(3, 1, 2).start()
+    load_w(2, 0, 2).wait()
+    down_all(0, 2, 0, 0)
+    load_w(0, 0, 2).start()
+    load_w(3, 1, 2).wait()
+    down_all(0, 3, 1, 1)
+    for q in range(n_tp):
+        give_back(0, q).start()
+    dispatch(1).wait_recv()
+    load_x(arrived.at[1], 1).start()
+    lax.fori_loop(4, 4 * n_ep, step_body, 0)
     keep_own().start()
     for q in range(1, n_tp):
         give_back(n_ep - 1, q).start()
 
-    for k in range(n_ep - 1):
+    for q in range(n_tp):
+        dispatch_first(q).wait_send()
+    for k in range(1, n_ep - 1):
         dispatch(k).wait_send()
     for a in range(3):
         core_copy(a).wait_send()
@@ -256,8 +348,8 @@
                    (dp, partner(k), source)).wait_recv()
 
 
-def run_layer(rows, wg, wu, wd):
-    n_ep, n_rows, d_model = rows.shape
+def run_layer(taken, x, n_rows, wg, wu, wd):
+    n_ep, d_model = taken.shape[0], x.shape[1]
     ff = wg.shape[2]
     quarter = d_model // 4
     bf16, dma = jnp.bfloat16, pltpu.SemaphoreType.DMA
@@ -265,32 +357,33 @@
         layer_kernel,
         name='moe_layer',
         out_shape=[jax.ShapeDtypeStruct((n_ep, 4, n_rows, quarter), bf16),
+                   jax.ShapeDtypeStruct((n_ep, n_rows, d_model), bf16),
                    jax.ShapeDtypeStruct((n_ep - 1, n_rows, d_model), bf16),
                    jax.ShapeDtypeStruct((3, d_model, ff), bf16),
                    jax.ShapeDtypeStruct((3, d_model, ff), bf16),
                    jax.ShapeDtypeStruct((3, ff, d_model), bf16)],
-        in_specs=[ANY] * 4,
-        out_specs=[ANY] * 5,
+        in_specs=[pl.BlockSpec(memory_space=pltpu.VMEM)] + [ANY] * 4,
+        out_specs=[ANY] * 6,
         scratch_shapes=[pltpu.VMEM((2, n_rows, d_model), bf16),
                         pltpu.VMEM((2, d_model, ff), bf16),
                         pltpu.VMEM((2, d_model, ff), bf16),
                         pltpu.VMEM((2, ff, d_model), bf16),
-                        pltpu.VMEM((n_rows, ff), bf16),
+                        pltpu.VMEM((2, n_rows, ff), bf16),
                         pltpu.VMEM((4, n_rows, quarter), jnp.float32),
                         pltpu.VMEM((n_ep, 4, n_rows, quarter), bf16),
-                        dma((2,)), dma((2, 3)), dma,
+                        dma((2,)), dma((2, 3)), dma, dma((4,)), dma((4,)), dma((4,)),
                         dma((n_ep - 1,)), dma((n_ep - 1,)), dma((3,)), dma((3,)),
                         *[dma((PIECES,)) for _ in range(8)],
                         dma((n_ep, 4)), dma((n_ep, 4))],
         compiler_params=pltpu.CompilerParams(has_side_effects=True, vmem_limit_bytes=VMEM_LIMIT),
-    )(rows, wg, wu, wd)
+    )(taken, x, wg, wu, wd)
     return outs[0]
 
 
 CHUNKS = 8
 
 
-def combine_kernel(first, second, gate0, gate1, results, out, wide, tile, done,
+def combine_kernel(first, second, gates, results, out, wide, tile0, tile1, done,
                    own_s, core_s, core_r, y_s, y_r, fwd_s, fwd_r):
     dp, z, tp = lax.axis_index('dp'), lax.axis_index('ep'), lax.axis_index('tp')
     y, c = tp // 2, tp % 2
@@ -326,21 +419,22 @@
 
     lax.fori_loop(0, 16, widen, 0)
     wide[pl.ds(n_res, 8), :] = jnp.zeros((8, cols), jnp.float32)
-    part = tile.shape[0]
+    part = tile0.shape[0]
 
     def part_body(i, carry):
         def eight(g, carry):
             for u in range(8):
-                local = g * 8 + u
-                t = i * part + local
-                row = gate0[t] * wide[pl.ds(first[t], 1), :] + gate1[t] * wide[pl.ds(second[t], 1), :]
-                tile[pl.ds(local, 1), :] = row
+                t = i * part + g * 8 + u
+                tile0[pl.ds(g * 8 + u, 1), :] = wide[pl.ds(first[t], 1), :]
+                tile1[pl.ds(g * 8 + u, 1), :] = wide[pl.ds(second[t], 1), :]
             return carry
 
         lax.fori_loop(0, part // 8, eight, 0)
         per = chunk // part
         b = i // per
-        done[b, pl.ds(pl.multiple_of(i % per * part, 16), part), :] = tile[...].astype(jnp.bfloat16)
+        weight = gates[pl.ds(pl.multiple_of(i * part, 8), part), :]
+        total = weight[:, 0:1] * tile0[...] + weight[:, 1:2] * tile1[...]
+        done[b, pl.ds(pl.multiple_of(i % per * part, 16), part), :] = total.astype(jnp.bfloat16)
 
         @pl.when(i % per == per - 1)
         def _():
@@ -373,14 +467,15 @@
         combine_kernel,
         name='moe_combine',
         out_shape=jax.ShapeDtypeStruct((tokens, 4 * cols), bf16),
-        in_specs=[smem] * 4 + [vmem],
+        in_specs=[smem] * 2 + [vmem] * 2,
         out_specs=ANY,
         scratch_shapes=[pltpu.VMEM((results.shape[0] + 8, cols), jnp.float32),
+                        pltpu.VMEM((min(256, chunk), cols), jnp.float32),
                         pltpu.VMEM((min(256, chunk), cols), jnp.float32),
                         pltpu.VMEM((CHUNKS, chunk, cols), bf16),
                         *[dma((CHUNKS,)) for _ in range(7)]],
         compiler_params=pltpu.CompilerParams(has_side_effects=True, vmem_limit_bytes=VMEM_LIMIT),
-    )(index[0], index[1], gates[0], gates[1], results)
+    )(index[0], index[1], gates, results)
 
 
 def solution(mesh):
@@ -393,23 +488,17 @@
         local_experts = wg_loc.shape[0]
         n_experts = local_experts * n_ep
         capacity = CAP_NUM * n_top * tokens // (CAP_DEN * n_experts)
-        half = capacity // 2
-        tp = lax.axis_index('tp')
-        parity, part = tp // 2, tp % 2
+        parity = lax.axis_index('tp') // 2
         chosen, slots = slot_numbers(ids_loc, n_experts)
         taken = jnp.where(chosen, slots, -1).reshape(n_ep, local_experts, tokens)
         taken = lax.dynamic_index_in_dim(taken, parity, axis=1, keepdims=False)
-        wanted = part * half + jnp.arange(half, dtype=jnp.int32)
-        number = jnp.arange(tokens, dtype=jnp.int32)
-        owner = jnp.max(jnp.where(taken[:, None, :] == wanted[None, :, None], number, 0), axis=2)
-        rows = jnp.take(x_loc, owner, axis=0, mode='clip')
         ids_t = ids_loc.T
         expert = jnp.arange(n_experts, dtype=jnp.int32)[None, :, None]
         copy_slot = jnp.sum(jnp.where(ids_t[:, None, :] == expert, slots[None], 0), axis=1)
         index = jnp.where(copy_slot < capacity, ids_t * capacity + copy_slot, n_experts * capacity)
-        results = run_layer(rows, wg_loc, wu_loc, wd_loc)
+        results = run_layer(taken.reshape(n_ep, tokens // 128, 128), x_loc, capacity // 2, wg_loc, wu_loc, wd_loc)
         results = results.reshape(n_experts * capacity, d_model // 4)
-        return run_combine(index, gates_loc.T, results)
+        return run_combine(index, gates_loc, results)
 
     return jax.shard_map(device_body, mesh=mesh,
                          in_specs=(row_spec, row_spec, row_spec, P('ep', None, 'tp'), P('ep', None, 'tp'), P('ep', 'tp', None)),

time: 657 us -> 623 us (0.948)
  local copies, waits for them, and re-layouts: 45.6 us -> 20.8 us
  other arithmetic: 8.85 us -> 1.87 us
    gather x1 -> x0, local copies, waits for them, and re-layouts: 28.3 us -> none  [device_body(): rows = jnp.take(x_loc, owner, axis=0, mode='clip')]
    reduce_max x1 -> x0, other arithmetic: 6.9 us -> none  [device_body(): jnp.max(jnp.where(taken[:, None, :] == wanted[None, :, None], number, 0),...]
    unnamed x3 -> x6, local copies, waits for them, and re-layouts: 14.3 us -> 19.1 us
where the time goes in v3:
time: 623 us
  Pallas kernels  600 us (96%)
  local copies, waits for them, and re-layouts  20.8 us (3%)
    pallas_call x1, Pallas kernels, run_layer(): pl.pallas_call(layer_kernel, name='moe_layer', out_shape=[jax.ShapeDtypeS...  491 us
    pallas_call x1, Pallas kernels, run_combine(): pl.pallas_call(combine_kernel, name='moe_combine', out_shape=jax.ShapeDty...  109 us
    unnamed x6, local copies, waits for them, and re-layouts  19.1 us

profile of v3, /device:TPU:0, one launch (start us, length us, event | category | flops | bytes accessed | tf_op | source)
XLA Modules:
  0.0 622.9 jit_solution(11621932374432834759)
XLA Ops:
  0.0 0.9 fusion.12
  0.9 0.1 fusion.4
  1.0 0.1 fusion.10
  1.1 0.2 fusion
  1.3 0.0 copy-start
  1.3 0.7 copy-done
  1.9 0.1 reshape.56
  2.0 0.1 constant_dynamic-slice_fusion
  2.1 0.1 fusion.5
  2.2 0.6 copy.20
  2.8 490.8 %moe_layer.1 = (bf16[4,4,640,512]{3,2,1,0:T(8,128)(2,1)}, bf16[4,640,2048]{2,1,0:T(8,128)(2,1)}, bf16[3,640,2048]{2,1,0:T(8,128)(2,1)}, bf16[3,2048,1408]{2,1,0:...) custom-call(s32[4,32,128]{2,1,0:T(8,128)} %bitcast.28, bf16[4096,2048]{1,0:T(8,128)(2,1)} %x.1, ...), custom_call_target="tpu_custom_call" | custom-call | tf_op jit(solution)/shard_map/moe_layer/pallas_call | solution.py:356
  493.7 1.0 copy.19
  494.6 0.9 select_reduce_fusion
  495.5 0.8 compare_select_fusion
  496.3 0.6 fusion.11
  496.9 2.7 copy.10.gates
  499.7 109.0 %moe_combine.1 = bf16[4096,2048]{1,0:T(8,128)(2,1)} custom-call(s32[4096]{0:T(1024)} %bitcast.36, s32[4096]{0:T(1024)} %bitcast.35, f32[4096,2]{1,0:T(8,128)} %copy.10.gates, bf16[10240,512]{1,0:T(8,128)(2,1)} %bitcast.24), custom_call_target="tpu_custom_call" | custom-call | tf_op jit(solution)/shard_map/moe_combine/pallas_call | solution.py:466
  608.7 14.2 %copy.22 = bf16[4096,2048]{1,0:T(8,128)(2,1)} copy(bf16[4096,2048]{1,0:T(8,128)(2,1)} %moe_combine.1) | data formatting | bytes 33554432
  (2 shorter events, 0.0 us)
Async XLA Ops:
  1.3 0.7 copy-start

commit v4 on v3

--- a/solution.py
+++ b/solution.py
@@ -152,13 +152,13 @@
 
             lax.fori_loop(0, half_t // 128, mark, 0)
 
-        @pl.when(k == 0)
-        def _():
+        def pick_cols(q, carry):
             for side in range(2):
-                for h in range(2):
-                    load_tokens(h, side).wait()
-
-        def pick_cols(q, carry):
+                @pl.when((k == 0) & (q == 2 * side))
+                def _():
+                    for h in range(2):
+                        load_tokens(h, side).wait()
+
             at = pl.ds(pl.multiple_of(q % 2 * quarter_cols, 128), quarter_cols)
             picked = [jnp.dot(xv.at[h][:, pl.ds(0, half_t)], w_vmem[h].at[q // 2][pl.ds(0, half_t), at],
                               preferred_element_type=jnp.float32) for h in range(2)]
@@ -380,11 +380,12 @@
     return outs[0]
 
 
-CHUNKS = 8
-
-
-def combine_kernel(first, second, gates, results, out, wide, tile0, tile1, done,
-                   own_s, core_s, core_r, y_s, y_r, fwd_s, fwd_r):
+CHUNKS = 16
+LOADS = 4
+
+
+def combine_kernel(first, second, gate0, gate1, results, out, held, wide, tile, done,
+                   load_s, own_s, core_s, core_r, y_s, y_r, fwd_s, fwd_r):
     dp, z, tp = lax.axis_index('dp'), lax.axis_index('ep'), lax.axis_index('tp')
     y, c = tp // 2, tp % 2
     n_res, cols = results.shape
@@ -410,31 +411,38 @@
     def forward(b):
         return remote(place(b, peer_chip), place(b, peer_chip), fwd_s.at[b], fwd_r.at[b], peer_core)
 
-    block = n_res // 16
+    load_rows = n_res // LOADS
+    block = load_rows // 4
+
+    def load(i):
+        at = pl.ds(i * load_rows, load_rows)
+        return pltpu.make_async_copy(results.at[at], held.at[at], load_s.at[i])
 
     def widen(r, carry):
         at = pl.ds(pl.multiple_of(r * block, 8), block)
-        wide[at, :] = results[at, :].astype(jnp.float32)
+        wide[at, :] = held[at, :].astype(jnp.float32)
         return carry
 
-    lax.fori_loop(0, 16, widen, 0)
+    for i in range(LOADS):
+        load(i).start()
     wide[pl.ds(n_res, 8), :] = jnp.zeros((8, cols), jnp.float32)
-    part = tile0.shape[0]
+    for i in range(LOADS):
+        load(i).wait()
+        lax.fori_loop(4 * i, 4 * i + 4, widen, 0)
+    part = tile.shape[0]
 
     def part_body(i, carry):
         def eight(g, carry):
             for u in range(8):
                 t = i * part + g * 8 + u
-                tile0[pl.ds(g * 8 + u, 1), :] = wide[pl.ds(first[t], 1), :]
-                tile1[pl.ds(g * 8 + u, 1), :] = wide[pl.ds(second[t], 1), :]
+                row = gate0[t] * wide[pl.ds(first[t], 1), :] + gate1[t] * wide[pl.ds(second[t], 1), :]
+                tile[pl.ds(g * 8 + u, 1), :] = row
             return carry
 
         lax.fori_loop(0, part // 8, eight, 0)
         per = chunk // part
         b = i // per
-        weight = gates[pl.ds(pl.multiple_of(i * part, 8), part), :]
-        total = weight[:, 0:1] * tile0[...] + weight[:, 1:2] * tile1[...]
-        done[b, pl.ds(pl.multiple_of(i % per * part, 16), part), :] = total.astype(jnp.bfloat16)
+        done[b, pl.ds(pl.multiple_of(i % per * part, 16), part), :] = tile[...].astype(jnp.bfloat16)
 
         @pl.when(i % per == per - 1)
         def _():
@@ -462,20 +470,19 @@
     chunk = tokens // CHUNKS
     bf16, dma = jnp.bfloat16, pltpu.SemaphoreType.DMA
     smem = pl.BlockSpec(memory_space=pltpu.SMEM)
-    vmem = pl.BlockSpec(memory_space=pltpu.VMEM)
     return pl.pallas_call(
         combine_kernel,
         name='moe_combine',
         out_shape=jax.ShapeDtypeStruct((tokens, 4 * cols), bf16),
-        in_specs=[smem] * 2 + [vmem] * 2,
+        in_specs=[smem] * 4 + [ANY],
         out_specs=ANY,
-        scratch_shapes=[pltpu.VMEM((results.shape[0] + 8, cols), jnp.float32),
-                        pltpu.VMEM((min(256, chunk), cols), jnp.float32),
+        scratch_shapes=[pltpu.VMEM(results.shape, bf16),
+                        pltpu.VMEM((results.shape[0] + 8, cols), jnp.float32),
                         pltpu.VMEM((min(256, chunk), cols), jnp.float32),
                         pltpu.VMEM((CHUNKS, chunk, cols), bf16),
-                        *[dma((CHUNKS,)) for _ in range(7)]],
+                        dma((LOADS,)), *[dma((CHUNKS,)) for _ in range(7)]],
         compiler_params=pltpu.CompilerParams(has_side_effects=True, vmem_limit_bytes=VMEM_LIMIT),
-    )(index[0], index[1], gates, results)
+    )(index[0], index[1], gates[0], gates[1], results)
 
 
 def solution(mesh):
@@ -498,7 +505,7 @@
         index = jnp.where(copy_slot < capacity, ids_t * capacity + copy_slot, n_experts * capacity)
         results = run_layer(taken.reshape(n_ep, tokens // 128, 128), x_loc, capacity // 2, wg_loc, wu_loc, wd_loc)
         results = results.reshape(n_experts * capacity, d_model // 4)
-        return run_combine(index, gates_loc, results)
+        return run_combine(index, gates_loc.T, results)
 
     return jax.shard_map(device_body, mesh=mesh,
                          in_specs=(row_spec, row_spec, row_spec, P('ep', None, 'tp'), P('ep', None, 'tp'), P('ep', 'tp', None)),

time: 623 us -> 617 us (level)
    unnamed x6 -> x3, local copies, waits for them, and re-layouts: 19.1 us -> 14.9 us
where the time goes in v4:
time: 617 us; the launch traced here: 616 us
  Pallas kernels  596 us (97%)
  local copies, waits for them, and re-layouts  18 us (3%)
    pallas_call x1, Pallas kernels, run_layer(): pl.pallas_call(layer_kernel, name='moe_layer', out_shape=[jax.ShapeDtypeS...  488 us
    pallas_call x1, Pallas kernels, run_combine(): pl.pallas_call(combine_kernel, name='moe_combine', out_shape=jax.ShapeDty...  108 us
    unnamed x3, local copies, waits for them, and re-layouts  14.9 us

profile of v4, /device:TPU:0, one launch (start us, length us, event | category | flops | bytes accessed | tf_op | source)
XLA Modules:
  0.0 616.2 jit_solution(14304683637610452468)
XLA Ops:
  0.0 1.5 fusion.11
  1.5 0.9 fusion.13
  2.3 0.1 fusion.4
  2.5 0.1 fusion.10
  2.6 0.2 fusion
  2.8 0.1 copy.17
  2.8 0.9 select_reduce_fusion
  3.7 0.8 compare_select_fusion
  4.5 0.6 fusion.12
  5.1 0.1 reshape.56
  5.2 0.1 constant_dynamic-slice_fusion
  5.3 0.1 fusion.5
  5.4 0.6 copy.18
  6.0 488.4 %moe_layer.1 = (bf16[4,4,640,512]{3,2,1,0:T(8,128)(2,1)}, bf16[4,640,2048]{2,1,0:T(8,128)(2,1)}, bf16[3,640,2048]{2,1,0:T(8,128)(2,1)}, bf16[3,2048,1408]{2,1,0:...) custom-call(s32[4,32,128]{2,1,0:T(8,128)} %bitcast.31, bf16[4096,2048]{1,0:T(8,128)(2,1)} %x.1, ...), custom_call_target="tpu_custom_call" | custom-call | tf_op jit(solution)/shard_map/moe_layer/pallas_call | solution.py:356
  494.5 107.6 %moe_combine.1 = bf16[4096,2048]{1,0:T(8,128)(2,1)} custom-call(s32[4096]{0:T(1024)} %bitcast.41, s32[4096]{0:T(1024)} %bitcast.40, f32[4096]{0:T(1024)} %bitcast.39, f32[4096]{0:T(1024)} %bitcast.38, bf16[10240,512]{1,0:T(8,128)(2,1)} %bitcast.27), custom_call_target="tpu_custom_call" | custom-call | tf_op jit(solution)/shard_map/moe_combine/pallas_call | solution.py:473
  602.1 14.2 %copy.20 = bf16[4096,2048]{1,0:T(8,128)(2,1)} copy(bf16[4096,2048]{1,0:T(8,128)(2,1)} %moe_combine.1) | data formatting | bytes 33554432
  (2 shorter events, 0.0 us)
